TPU v7x, 512 devices: a whole 4x4x16 slice. The times are simulated.
512 devices in a mesh: grp: 16 (over y, z_hi, core), dev: 32 (over z_lo, x).
Axes of the slice: x: 4, y: 4, z: 16 (z_hi: 2, z_lo: 8; z = z_hi * 8 + z_lo), core: 2. Of those that a mesh axis runs over, the one named last changes fastest.
Arguments:
- train_grads: bfloat16 [65536, 1024], P(('grp', 'dev')), may hold values from -192 to 192, as said below
- queries: bfloat16 [2048, 1024], P('grp'), may hold values from -6 to 6
Outputs:
- scores: bfloat16 [65536, 2048], P(('grp', 'dev'))
Inputs may be any that keep to these rules, and one draw needn't show every extreme that they name: `train_grads`: Real-valued projected gradients whose columns and rows differ in scale.
All inputs are finite; a program needn't handle non-finite values. Where the computation divides by a largest or mean magnitude, that divisor is 1e-20 or more.
Results may differ from a plain program's by a relative error of at most 0.001.
The roundings to bfloat16 on the way count: a program that leaves them out, or rounds other values in their place, can miss the bound.
Values may be sent and summed in bfloat16 or wider, within the bound.
A program may use at most 64 MiB of HBM per device.

v0:
```python
import jax
import jax.numpy as jnp
from jax import lax
from jax.sharding import PartitionSpec as P

ITERS = 8
damping_ratio = 0.1


def copy_for_each(array, axis):
    copies = jnp.broadcast_to(array, (lax.axis_size(axis), *array.shape))
    return lax.all_to_all(copies, axis, split_axis=0, concat_axis=0, tiled=True)


def laid_out(pieces, dim):
    dims = list(pieces.shape[1:])
    dims[dim] *= pieces.shape[0]
    return jnp.moveaxis(pieces, 0, dim).reshape(dims)


def gather_directly(array, axis, dim):
    pieces = copy_for_each(array, axis)
    return laid_out(pieces, dim)


def local_solve(gram, own, total, width):
    normed = gram / total
    damp = damping_ratio * jnp.trace(gram) / (total * width)
    bound = jnp.max(jnp.sum(jnp.abs(normed), axis=1)) + damp
    step = 1.0 / bound
    oper = normed + damp * jnp.eye(width, dtype=jnp.float32)
    state = step * own
    for index in range(ITERS):
        state = state + step * (own - jnp.dot(state, oper, precision=lax.Precision.HIGHEST))
    return state.astype(jnp.bfloat16)


def body(train_grads, queries):
    rows, width = train_grads.shape
    ndevice = lax.axis_size("dev")
    total = rows * ndevice * lax.axis_size("grp")
    qvals = queries.astype(jnp.float32)
    qrows = qvals.shape[0] // ndevice
    qstart = lax.axis_index("dev") * qrows
    own = lax.dynamic_slice_in_dim(qvals, qstart, qrows, 0)
    gram = lax.psum(
        lax.dot_general(
            train_grads, train_grads, (((0,), (0,)), ((), ())), preferred_element_type=jnp.float32
        ),
        ("grp", "dev"),
    )
    mine = local_solve(gram, own, total, width)
    prepared = gather_directly(mine, "dev", 0)
    return lax.dot_general(
        train_grads,
        lax.all_gather(prepared, "grp", axis=0, tiled=True),
        (((1,), (1,)), ((), ())),
        preferred_element_type=jnp.float32,
    ).astype(jnp.bfloat16)


def solution(mesh):
    return jax.shard_map(
        body,
        mesh=mesh,
        in_specs=(P(("grp", "dev"), None), P("grp", None)),
        out_specs=P(("grp", "dev"), None),
        check_vma=False,
    )
```

profile of v0, /device:TPU:1, one launch (start us, length us, event | category | flops | bytes accessed | tf_op | source)
XLA Modules:
  0.0 696.8 jit_solution(398364279938283323)
XLA Ops:
  6.5 0.0 copy-start
  6.5 0.0 all-reduce.2.cloned.1.call-start
  6.5 0.9 copy-done
  7.5 2.7 fusion.19
  10.2 0.0 all-reduce.2.cloned.1.call-update
  10.2 0.0 all-gather.2.cloned.1.call-start
  10.3 500.9 %all-reduce.2.cloned.1.call-done = f32[1024,1024]{1,0:T(8,128)} async-done(((f32[1024,1024]{1,0:T(8,128)}), f32[1024,1024]{1,0:T(8,128)}) %all-reduce.2.cloned.1.call-update) | async-done | bytes 4194320 | tf_op jit(solution)/shard_map/psum | solution.py:46
  511.2 3.3 select_reduce_fusion
  515.2 0.6 reduce_max.9
  516.5 4.6 fusion.16
  521.1 3.0 fusion.14
  524.1 3.0 fusion.12
  527.0 3.0 fusion.10
  530.0 3.0 fusion.8
  532.9 3.1 fusion.6
  536.1 3.0 fusion.4
  539.0 3.0 fusion.17
  542.0 0.1 broadcast_in_dim.8
  542.1 31.9 %all_to_all.5 = bf16[32,4,1024]{2,1,0:T(4,128)(2,1)S(1)} all-to-all(bf16[32,4,1024]{2,1,0:T(4,128)(2,1)S(1)} %broadcast_in_dim.8), channel_id=1, replica_groups=mesh['grp'=16,'dev'=32] {'dev'}, dimensions={0} | all-to-all | bytes 524288 | tf_op jit(solution)/shard_map/all_to_all | solution.py:12
  574.0 0.8 reshape.3
  574.8 0.0 all-gather.2.cloned.1.call-update
  574.8 110.7 %all-gather.2.cloned.1.call-done = bf16[2048,1024]{1,0:T(8,128)(2,1)} async-done(((bf16[128,1024]{1,0:T(8,128)(2,1)}), bf16[2048,1024]{1,0:T(8,128)(2,1)}) %all-gather.2.cloned.1.call-update) | async-done | bytes 4194320 | tf_op jit(solution)/shard_map/all_gather | solution.py:56
  685.5 3.4 fusion
  689.0 1.0 copy.3
  (2 shorter events, 0.0 us)
Async XLA Ops:
  6.5 1.0 copy-start
  6.5 504.7 %all-reduce.2.cloned.1.call-start = ((), (), s32[]{:S(2)}) async-start(), calls=%async_computation.1 | async-start | bytes 8388608 | tf_op jit(solution)/shard_map/psum | solution.py:46
  10.2 675.3 %all-gather.2.cloned.1.call-start = ((), (), s32[]{:S(2)}) async-start(), calls=%async_computation.2 | async-start | bytes 4456448 | tf_op jit(solution)/shard_map/all_gather | solution.py:56
  516.5 4.6 copy-start.1
Sparse Core Ops, SparseCore 0:
  12.8 498.3 all-reduce.1
  574.9 110.5 all-gather.1
where the time goes:
time: 698 us; the launch traced here: 697 us
  waiting for transfers between devices  612 us (88%)
  blocking collectives  31.9 us (5%)
  matrix products  31.6 us (5%)
  between operations  14.8 us (2%)
    psum x1, waiting for transfers between devices, body(): lax.psum(lax.dot_general(train_grads, train_grads, (((0,), (0,)), ((), ()...  501 us
    all_gather x1, waiting for transfers between devices, body(): lax.all_gather(prepared, 'grp', axis=0, tiled=True)  111 us
    all_to_all x1, blocking collectives, copy_for_each(): return lax.all_to_all(copies, axis, split_axis=0, concat_axis=0, tiled=True)  31.9 us
    dot_general x8, matrix products, local_solve(): jnp.dot(state, oper, precision=lax.Precision.HIGHEST)  25.5 us
  transfers between devices with their start and end apart: 2, of which 2 were waited for; matrix products, arithmetic and copies ran while one was open for 0% of the time, Pallas kernels for 0%

commit v1 on v0

--- a/solution.py
+++ b/solution.py
@@ -51,9 +51,18 @@
     )
     mine = local_solve(gram, own, total, width)
     prepared = gather_directly(mine, "dev", 0)
+    work_field_by_axis = lambda xx, bus_axis: jnp.concatenate(
+        lax.all_to_all(
+            jnp.stack([xx for _ in range(lax.axis_size(bus_axis))]),
+            axis_name=bus_axis,
+            split_axis=0,
+            concat_axis=0,
+        ),
+        axis=0,
+    )
     return lax.dot_general(
         train_grads,
-        lax.all_gather(prepared, "grp", axis=0, tiled=True),
+        work_field_by_axis(prepared, "grp"),
         (((1,), (1,)), ((), ())),
         preferred_element_type=jnp.float32,
     ).astype(jnp.bfloat16)

time: 698 us -> 782 us (1.12)
  the two profiles are of different devices: /device:TPU:1 before, /device:TPU:32 now
where the time goes in v1:
time: 782 us; the launch traced here: 781 us
  waiting for transfers between devices  499 us (64%)
  blocking collectives  231 us (30%)
  matrix products  29.4 us (4%)
  between operations  14.8 us (2%)
    psum x1, waiting for transfers between devices, body(): lax.psum(lax.dot_general(train_grads, train_grads, (((0,), (0,)), ((), ()...  499 us
    all_to_all x1, blocking collectives, body(): lax.all_to_all(jnp.stack([xx for _ in range(lax.axis_size(bus_axis))]), a...  203 us
    all_to_all x1, blocking collectives, copy_for_each(): return lax.all_to_all(copies, axis, split_axis=0, concat_axis=0, tiled=True)  28.3 us
    dot_general x8, matrix products, local_solve(): jnp.dot(state, oper, precision=lax.Precision.HIGHEST)  25.5 us
  transfers between devices with their start and end apart: 1, of which 1 were waited for; matrix products, arithmetic and copies ran while one was open for 0% of the time, Pallas kernels for 0%

profile of v1, /device:TPU:32, one launch (start us, length us, event | category | flops | bytes accessed | tf_op | source)
XLA Modules:
  0.0 781.3 jit_solution(8021927225910108518)
XLA Ops:
  6.5 0.0 copy-start
  6.5 0.0 all-reduce.2.cloned.1.call-start
  6.5 0.9 copy-done
  7.5 2.7 fusion.19
  10.2 0.0 all-reduce.2.cloned.1.call-update
  10.2 499.5 %all-reduce.2.cloned.1.call-done = f32[1024,1024]{1,0:T(8,128)} async-done(((f32[1024,1024]{1,0:T(8,128)}), f32[1024,1024]{1,0:T(8,128)}) %all-reduce.2.cloned.1.call-update) | async-done | bytes 4194320 | tf_op jit(solution)/shard_map/psum | solution.py:46
  509.7 3.3 select_reduce_fusion
  513.7 0.6 reduce_max.9
  514.9 0.0 copy-start.1
  515.0 4.6 fusion.16
  519.6 3.0 fusion.14
  522.5 3.0 fusion.12
  525.5 3.0 fusion.10
  528.4 3.0 fusion.8
  531.4 3.1 fusion.6
  534.5 3.0 fusion.4
  537.5 3.0 fusion.17
  540.5 0.1 broadcast_in_dim.8
  540.6 28.3 %all_to_all.10 = bf16[32,4,1024]{2,1,0:T(4,128)(2,1)S(1)} all-to-all(bf16[32,4,1024]{2,1,0:T(4,128)(2,1)S(1)} %broadcast_in_dim.8), channel_id=1, replica_groups=mesh['grp'=16,'dev'=32] {'dev'}, dimensions={0} | all-to-all | bytes 524288 | tf_op jit(solution)/shard_map/all_to_all | solution.py:12
  568.9 0.1 stack_reshape.2
  568.9 0.5 stack.3
  569.5 202.7 %all_to_all.11 = bf16[16,128,1024]{2,1,0:T(8,128)(2,1)S(1)} all-to-all(bf16[16,128,1024]{2,1,0:T(8,128)(2,1)S(1)} %stack.3), channel_id=1, replica_groups=mesh['grp'=16,'dev'=32] {'grp'}, dimensions={0} | all-to-all | bytes 8388608 | tf_op jit(solution)/shard_map/all_to_all | solution.py:55
  772.2 1.3 fusion
  773.4 1.0 copy.3
  (1 shorter events, 0.0 us)
Async XLA Ops:
  6.5 1.0 copy-start
  6.5 503.1 %all-reduce.2.cloned.1.call-start = ((), (), s32[]{:S(2)}) async-start(), calls=%async_computation.2 | async-start | bytes 8388608 | tf_op jit(solution)/shard_map/psum | solution.py:46
  514.9 4.6 copy-start.1
Sparse Core Ops, SparseCore 0:
  12.8 496.8 all-reduce.1
